TPU v7x, 32 devices: a whole 2x2x4 slice. The times are simulated.
32 devices in a mesh: slab: 8 (over z, y), pencil: 4 (over x, core).
Axes of the slice: x: 2, y: 2, z: 4, core: 2. Of those that a mesh axis runs over, the one named last changes fastest.
Arguments:
- density_history: float32 [7, 64, 320, 320], P(None, 'slab', 'pencil'), may hold values from -6 to 6
- residual_history: float32 [7, 64, 320, 320], P(None, 'slab', 'pencil'), as said below
- occupancy_history: float32 [7, 768, 324], P(None, ('slab', 'pencil')), may hold values from -6 to 6
- occupancy_residual: float32 [7, 768, 324], P(None, ('slab', 'pencil')), may hold values from -6 to 6
- species: int32 [768], P(('slab', 'pencil')), may hold values from 0 to 3
- slot_count: int32 [32], P(('slab', 'pencil')), may hold values from 12 to 24, as said below
Outputs:
- new_density: float32 [64, 320, 320], P('slab', 'pencil')
- new_occupancy: float32 [768, 324], P(('slab', 'pencil'))
Inputs may be any that keep to these rules, and one draw needn't show every extreme that they name: `residual_history`: residual fields of the 7 previous steps. Device d of slab+pencil (slab slowest) holds slots d * 24 to (d + 1) * 24 - 1, of which the first slot_count[d] hold atoms; some device is full in every draw.
All inputs are finite; a program needn't handle non-finite values.
Results may differ from a plain program's by a relative error of at most 0.00017.
Values sent between devices are 32-bit elements; how exact they have to be, the bound alone decides.
A program may use at most 128 MiB of HBM per device.

v0:
```python
import functools
import math

import jax
import jax.numpy as jnp
import numpy as np
from jax import lax
from jax.experimental import pallas as pl
from jax.experimental.pallas import tpu as pltpu
from jax.sharding import PartitionSpec as P

ORBITALS = 18


highest = lax.Precision.HIGHEST
grid_mixing = 0.5
block_mixing = 0.5
kerker_wave = 6.0
species_orbitals = (18, 13, 8, 5)


def block_mask(species, slot_count):
    live = jnp.arange(species.shape[0], dtype=jnp.int32) < slot_count[0]
    orbitals = jnp.zeros_like(species)
    for species_index, orbital_number in enumerate(species_orbitals):
        orbitals = orbitals + orbital_number * (species == species_index).astype(jnp.int32)
    entry = jnp.arange(ORBITALS * ORBITALS, dtype=jnp.int32)
    row_index = entry // ORBITALS
    column_index = entry % ORBITALS
    inside = (
        (row_index[None, :] < orbitals[:, None])
        & (column_index[None, :] < orbitals[:, None])
        & live[:, None]
    )
    return inside.astype(jnp.float32)


def mixing_weights(intersection):
    factor = jnp.linalg.cholesky(intersection)
    column = jnp.ones((intersection.shape[0], 1), intersection.dtype)
    middle = lax.linalg.triangular_solve(factor, column, left_side=True, lower=True)
    solved = lax.linalg.triangular_solve(
        factor, middle, left_side=True, lower=True, transpose_a=True
    )
    return solved[:, 0] / jnp.sum(solved)


def cosine_sine(length, freq_index, space_index):
    product = freq_index * space_index % length
    angle = 2.0 * math.pi / length * product.astype(jnp.float32)
    return (jnp.cos(angle), jnp.sin(angle))


def forward_spectra(fields, pencil_move, slab_move):
    batches, z_local, y_local, x_length = fields.shape
    pencil_count = lax.axis_size("pencil")
    slab_count = lax.axis_size("slab")
    x_columns = x_length // 2
    kx_local = x_columns // pencil_count
    y_length = y_local * pencil_count
    ky_local = y_length // slab_count
    z_length = z_local * slab_count
    freq_index = jnp.arange(x_columns, dtype=jnp.int32).reshape(pencil_count, kx_local, 1)
    space_index = jnp.arange(x_length, dtype=jnp.int32).reshape(1, 1, x_length)
    cosine, sine = cosine_sine(x_length, freq_index, space_index)
    nyquist = cosine_sine(x_length, jnp.full((1, 1, 1), x_length // 2, jnp.int32), space_index)[0]
    sine = jnp.where(freq_index == 0, -nyquist, sine)
    real_part = jnp.einsum("bzyx,pkx->bpkzy", fields, cosine, precision=highest)
    imag_part = -jnp.einsum("bzyx,pkx->bpkzy", fields, sine, precision=highest)
    packed = jnp.stack((real_part, imag_part), axis=1).reshape(batches, 2, pencil_count, -1)
    moved = pencil_move(packed).reshape(batches, 2, pencil_count, kx_local, z_local, y_local)
    freq_index = jnp.arange(y_length, dtype=jnp.int32).reshape(slab_count, ky_local, 1, 1)
    space_index = jnp.arange(y_length, dtype=jnp.int32).reshape(1, 1, pencil_count, y_local)
    cosine, sine = cosine_sine(y_length, freq_index, space_index)
    real_input = moved[:, 0]
    imag_input = moved[:, 1]
    form = "bskzy,glsy->bgklz"
    real_part = jnp.einsum(form, real_input, cosine, precision=highest) + jnp.einsum(
        form, imag_input, sine, precision=highest
    )
    imag_part = jnp.einsum(form, imag_input, cosine, precision=highest) - jnp.einsum(
        form, real_input, sine, precision=highest
    )
    packed = jnp.stack((real_part, imag_part), axis=1).reshape(batches, 2, slab_count, -1)
    moved = slab_move(packed).reshape(batches, 2, slab_count, kx_local, ky_local, z_local)
    freq_index = jnp.arange(z_length, dtype=jnp.int32).reshape(z_length, 1, 1)
    space_index = jnp.arange(z_length, dtype=jnp.int32).reshape(1, slab_count, z_local)
    cosine, sine = cosine_sine(z_length, freq_index, space_index)
    real_input = moved[:, 0]
    imag_input = moved[:, 1]
    form = "bgklz,mgz->bklm"
    real_part = jnp.einsum(form, real_input, cosine, precision=highest) + jnp.einsum(
        form, imag_input, sine, precision=highest
    )
    imag_part = jnp.einsum(form, imag_input, cosine, precision=highest) - jnp.einsum(
        form, real_input, sine, precision=highest
    )
    return jnp.stack((real_part, imag_part), axis=1)


def magnitude(index, length):
    return jnp.minimum(index, length - index).astype(jnp.float32)


def kerker_factor(freq_x, ky_local, x_length, y_length, z_length):
    freq_y = lax.axis_index("slab") * ky_local + jnp.arange(ky_local, dtype=jnp.int32)
    freq_z = jnp.arange(z_length, dtype=jnp.int32)
    square = (
        magnitude(freq_x, x_length)[:, None, None] ** 2
        + magnitude(freq_y, y_length)[None, :, None] ** 2
        + magnitude(freq_z, z_length)[None, None, :] ** 2
    )
    return square / (square + kerker_wave * kerker_wave)


def inverse_field(spectrum, z_local, y_local, x_length):
    pencil_count = lax.axis_size("pencil")
    slab_count = lax.axis_size("slab")
    x_columns = x_length // 2
    kx_local = x_columns // pencil_count
    slots = spectrum.shape[1]
    y_length = y_local * pencil_count
    ky_local = y_length // slab_count
    z_length = z_local * slab_count
    freq_index = jnp.arange(z_length, dtype=jnp.int32).reshape(z_length, 1, 1)
    space_index = jnp.arange(z_length, dtype=jnp.int32).reshape(1, slab_count, z_local)
    cosine, sine = cosine_sine(z_length, freq_index, space_index)
    real_input = spectrum[0]
    imag_input = spectrum[1]
    form = "klm,mdz->dklz"
    real_part = jnp.einsum(form, real_input, cosine, precision=highest) - jnp.einsum(
        form, imag_input, sine, precision=highest
    )
    imag_part = jnp.einsum(form, real_input, sine, precision=highest) + jnp.einsum(
        form, imag_input, cosine, precision=highest
    )
    packed = jnp.stack((real_part, imag_part), axis=0).reshape(2, slab_count, -1)
    moved = lax.all_to_all(packed, "slab", split_axis=1, concat_axis=1, tiled=True).reshape(
        2, slab_count, slots, ky_local, z_local
    )
    freq_index = jnp.arange(y_length, dtype=jnp.int32).reshape(slab_count, ky_local, 1, 1)
    space_index = jnp.arange(y_length, dtype=jnp.int32).reshape(1, 1, pencil_count, y_local)
    cosine, sine = cosine_sine(y_length, freq_index, space_index)
    real_input = moved[0]
    imag_input = moved[1]
    form = "gklz,glqy->qkzy"
    real_part = jnp.einsum(form, real_input, cosine, precision=highest) - jnp.einsum(
        form, imag_input, sine, precision=highest
    )
    imag_part = jnp.einsum(form, real_input, sine, precision=highest) + jnp.einsum(
        form, imag_input, cosine, precision=highest
    )
    packed = jnp.stack((real_part, imag_part), axis=0).reshape(2, pencil_count, -1)
    moved = lax.all_to_all(packed, "pencil", split_axis=1, concat_axis=1, tiled=True).reshape(
        2, pencil_count, slots, z_local, y_local
    )
    pencil_index = jnp.arange(pencil_count, dtype=jnp.int32).reshape(pencil_count, 1, 1)
    slot_index = jnp.arange(slots, dtype=jnp.int32).reshape(1, slots, 1)
    space_index = jnp.arange(x_length, dtype=jnp.int32).reshape(1, 1, x_length)
    freq_index = pencil_index * kx_local + slot_index
    cosine, sine = cosine_sine(x_length, freq_index, space_index)
    nyquist = cosine_sine(x_length, jnp.full((1, 1, 1), x_length // 2, jnp.int32), space_index)[0]
    ordinary = slot_index < kx_local
    doubling = jnp.where(freq_index == 0, 1.0, 2.0)
    real_table = jnp.where(ordinary, doubling * cosine, 0.0)
    imag_table = jnp.where(ordinary, -doubling * sine, jnp.where(pencil_index == 0, nyquist, 0.0))
    form = "pkzy,pkx->zyx"
    field = jnp.einsum(form, moved[0], real_table, precision=highest) + jnp.einsum(
        form, moved[1], imag_table, precision=highest
    )
    return field / (x_length * y_length * z_length)


def body(
    density_history, residual_history, occupancy_history, occupancy_residual, species, slot_count
):
    histories, z_local, y_local, x_length = residual_history.shape
    slab_count = lax.axis_size("slab")
    pencil_count = lax.axis_size("pencil")
    cell_total = z_local * slab_count * y_local * pencil_count * x_length
    slot_total = species.shape[0] * slab_count * pencil_count
    mask = block_mask(species, slot_count)
    flat = residual_history.reshape(histories, -1)
    grid_local = jnp.dot(flat, flat.T, precision=highest) / cell_total
    blocks = (occupancy_residual * mask[None]).reshape(histories, -1)
    block_local = jnp.dot(blocks, blocks.T, precision=highest) / (100.0 * slot_total)
    grid_intersection, block_intersection = lax.psum((grid_local, block_local), ("slab", "pencil"))
    weights = mixing_weights(grid_intersection + block_intersection)
    mixed = jnp.tensordot(weights, residual_history, axes=1, precision=highest)
    spectrum = forward_spectra(
        mixed[None],
        lambda packed: lax.all_to_all(packed, "pencil", split_axis=2, concat_axis=2, tiled=True),
        lambda packed: lax.all_to_all(packed, "slab", split_axis=2, concat_axis=2, tiled=True),
    )[0]
    x_columns = x_length // 2
    kx_local = x_columns // pencil_count
    y_length = y_local * pencil_count
    z_length = z_local * slab_count
    ky_local = y_length // slab_count
    freq_x = lax.axis_index("pencil") * kx_local + jnp.arange(kx_local, dtype=jnp.int32)
    factor = kerker_factor(freq_x, ky_local, x_length, y_length, z_length)
    filtered_spectrum = spectrum * factor[None]
    nyquist_x = jnp.full((1,), x_length // 2, jnp.int32)
    nyquist_factor = kerker_factor(nyquist_x, ky_local, x_length, y_length, z_length)
    owner = (lax.axis_index("pencil") == 0).astype(jnp.float32)
    extra = spectrum[:, 0:1] * nyquist_factor[None] * owner
    filtered_spectrum = jnp.concatenate((filtered_spectrum, extra), axis=1)
    filtered = inverse_field(filtered_spectrum, z_local, y_local, x_length)
    new_density = (
        jnp.tensordot(weights, density_history, axes=1, precision=highest) + grid_mixing * filtered
    )
    mixed_blocks = jnp.tensordot(
        weights, occupancy_history + block_mixing * occupancy_residual, axes=1, precision=highest
    )
    return (new_density, mask * mixed_blocks)


MESH = pl.DeviceIdType.MESH


def split(value):
    high = value.astype(jnp.bfloat16)
    low = (value - high.astype(jnp.float32)).astype(jnp.bfloat16)
    return high, low


def three(left, right, dims):
    numbers = (dims, ((), ()))
    dot = functools.partial(
        lax.dot_general, dimension_numbers=numbers, preferred_element_type=jnp.float32
    )
    return dot(left[1], right[0]) + dot(left[0], right[1]) + dot(left[0], right[0])


def halves(table):
    table = np.asarray(table, np.float32)
    high = table.astype(jnp.bfloat16)
    low = (table - high.astype(np.float32)).astype(jnp.bfloat16)
    return np.stack((high, low))


def waves(rows, columns, length):
    angle = 2.0 * np.pi / length * (np.outer(rows, columns) % length)
    return np.cos(angle), np.sin(angle)


def tables(x_length, y_length, z_length, pencil_count, slab_count):
    columns = x_length // 2
    cosine, sine = waves(np.arange(columns), np.arange(x_length), x_length)
    nyquist = np.where(np.arange(x_length) % 2 == 0, 1.0, -1.0)
    imag = -sine
    imag[0] = nyquist
    slots_k = columns // (pencil_count * slab_count)
    owner, slot = np.arange(columns) // slots_k, np.arange(columns) % slots_k
    chunk = np.searchsorted(cuts_of(slots_k), slot, side="right")
    order = np.lexsort((slot, owner, chunk))
    x_forward = np.stack((cosine, imag), axis=1)[order].reshape(x_length, x_length)
    doubling = np.where(np.arange(columns) == 0, 1.0, 2.0)[:, None]
    back = np.stack((doubling * cosine, doubling * imag), axis=1)[order]
    back = back.reshape(x_length, x_length)
    x_back = back * (grid_mixing / (x_length * y_length * z_length))
    cosine, sine = waves(np.arange(y_length), np.arange(y_length), y_length)
    along_y = np.stack((cosine, sine))
    cosine, sine = waves(np.arange(z_length), np.arange(z_length), z_length)
    order = np.arange(z_length).reshape(slab_count, -1).T.reshape(-1)
    cosine, sine = cosine[:, order], sine[:, order]
    z_forward = np.block([[cosine, sine], [-sine, cosine]])
    z_back = np.block([[cosine.T, -sine.T], [sine.T, cosine.T]])
    return [halves(t) for t in (x_forward, x_back, along_y, z_forward, z_back)]


def cuts_of(slots):
    return [at for at in range(1, slots, 2)] + [slots]


def pairs_of(count):
    return [(i, j) for i in range(count) for j in range(i + 1)]


def solve_weights(entry, count):
    lower, pivot = {}, []
    for j in range(count):
        scaled = [lower[j, k] * pivot[k] for k in range(j)]
        value = entry[j, j]
        for k in range(j):
            value = value - lower[j, k] * scaled[k]
        pivot.append(value)
        for i in range(j + 1, count):
            value = entry[i, j]
            for k in range(j):
                value = value - lower[i, k] * scaled[k]
            lower[i, j] = value / pivot[j]
    middle = []
    for i in range(count):
        value = jnp.ones_like(pivot[0])
        for k in range(i):
            value = value - lower[i, k] * middle[k]
        middle.append(value)
    solved = [None] * count
    for i in reversed(range(count)):
        value = middle[i] / pivot[i]
        for k in range(i + 1, count):
            value = value - lower[k, i] * solved[k]
        solved[i] = value
    total = solved[0]
    for value in solved[1:]:
        total = total + value
    return [value / total for value in solved]


def mix_kernel(
    slabs, pencils, cells, slots,
    res_hbm, dens_hbm, occ_ref, occ_res_ref, species_ref, live_ref, corner_ref,
    xf_hbm, yt_hbm, zf_hbm, zb_hbm,
    out_ref, occ_out_ref, field,
    res, dens, sums, send_box, land_box, planes, spectrum, back_box,
    xf_ref, yt_ref, zf_ref, zb_ref,
    load_sem, table_sem, sum_send, sum_recv, go_send, go_recv, back_send, back_recv,
):
    devices = slabs * pencils
    count, z_local, y_local, x_length = res.shape
    slots_k = x_length // 2 // devices
    freqs = 2 * slots_k
    z_length = z_local * slabs
    y_length = y_local * pencils
    tiles_out = send_box.shape[0]
    slab = lax.axis_index("slab")
    pencil = lax.axis_index("pencil")
    me = slab * pencils + pencil
    pairs = pairs_of(count)

    def place(index):
        return (lax.div(index, pencils), lax.rem(index, pencils))

    def other(step):
        return lax.rem(me + step, devices)

    barrier = pltpu.get_barrier_semaphore()

    def greet(step, _):
        pl.semaphore_signal(
            barrier, inc=1, device_id=place(other(step)), device_id_type=MESH
        )
        return 0

    lax.fori_loop(1, devices, greet, 0)

    def load(source, target, which, z):
        return pltpu.make_async_copy(source.at[:, z], target.at[:, z], load_sem.at[which, z])

    for z in range(z_local):
        load(res_hbm, res, 0, z).start()
    from_tables = (xf_hbm, yt_hbm, zf_hbm, zb_hbm)
    to_tables = (xf_ref, yt_ref, zf_ref, zb_ref)
    loads = [
        pltpu.make_async_copy(a, b, table_sem.at[at])
        for at, (a, b) in enumerate(zip(from_tables, to_tables))
    ]
    for copy in loads:
        copy.start()
    for z in range(z_local):
        load(dens_hbm, dens, 1, z).start()

    limit_shape = (occ_ref.shape[1], 1)
    slot_index = lax.broadcasted_iota(jnp.int32, limit_shape, 0)
    limit = jnp.zeros(limit_shape, jnp.int32)
    for slot in range(occ_ref.shape[1]):
        orbitals = jnp.int32(0)
        for species_index, orbital_number in enumerate(species_orbitals):
            orbitals = jnp.where(species_ref[slot] == species_index, orbital_number, orbitals)
        orbitals = jnp.where(slot < live_ref[0], orbitals, 0)
        limit = jnp.where(slot_index == slot, orbitals, limit)
    mask = (corner_ref[...] < limit).astype(jnp.float32)
    blocks = [occ_res_ref[i] * mask for i in range(count)]
    totals = [
        jnp.sum(blocks[i] * blocks[j], keepdims=True) / (100.0 * slots) for i, j in pairs
    ]
    whole = x_length // 128
    rest = x_length - whole * 128
    for first, width, tiles in ((0, 128, whole), (whole * 128, rest, 1 if rest else 0)):
        if tiles == 0:
            continue
        acc = [jnp.zeros((8, width), jnp.float32) for _ in pairs]
        for z in range(z_local):
            if first == 0:
                load(res_hbm, res, 0, z).wait()

            def rows(step, acc):
                acc = list(acc)
                row = pl.multiple_of(step * 8, 8)
                for t in range(tiles):
                    lane = first + 128 * t
                    part = [res[i, z, pl.ds(row, 8), lane:lane + width] for i in range(count)]
                    for at, (i, j) in enumerate(pairs):
                        acc[at] = acc[at] + part[i] * part[j]
                return tuple(acc)

            acc = lax.fori_loop(0, y_local // 8, rows, tuple(acc))
        totals = [t + jnp.sum(a, keepdims=True) / cells for t, a in zip(totals, acc)]
    lane_index = lax.broadcasted_iota(jnp.int32, (1, 128), 1)
    packed = jnp.zeros((1, 128), jnp.float32)
    for at, value in enumerate(totals):
        packed = jnp.where(lane_index == at, value, packed)
    sums[me] = packed

    pl.semaphore_wait(barrier, devices - 1)

    def sum_copy(step, source):
        return pltpu.make_async_remote_copy(
            src_ref=sums.at[source], dst_ref=sums.at[source],
            send_sem=sum_send.at[step], recv_sem=sum_recv.at[source],
            device_id=place(other(step)), device_id_type=MESH,
        )

    def start_sum(step, _):
        sum_copy(step, me).start()
        return 0

    def wait_sum(step, _):
        sum_copy(step, other(step)).wait_recv()
        return 0

    def drain_sum(step, _):
        sum_copy(step, me).wait_send()
        return 0

    lax.fori_loop(1, devices, start_sum, 0)
    lax.fori_loop(1, devices, wait_sum, 0)
    gathered = sums[0]
    for d in range(1, devices):
        gathered = gathered + sums[d]
    entry = {
        pair: jnp.sum(jnp.where(lane_index == at, gathered, 0.0), axis=1, keepdims=True)
        for at, pair in enumerate(pairs)
    }
    weights = solve_weights(entry, count)

    loads[0].wait()
    mixture = []
    for z in range(z_local):
        total = weights[0] * res[0, z]
        for i in range(1, count):
            total = total + weights[i] * res[i, z]
        mixture.append(total)
    mixture = split(jnp.concatenate(mixture, axis=0))
    ends = cuts_of(slots_k)
    chunks = list(zip([0] + ends[:-1], ends))

    def share(chunk, index):
        first, end = chunks[chunk]
        size = 2 * (end - first)
        return pl.ds(2 * first * devices + index * size, size)

    def go_copy(chunk, step, source, target):
        return pltpu.make_async_remote_copy(
            src_ref=send_box.at[:, share(chunk, target), :],
            dst_ref=land_box.at[:, share(chunk, source), :],
            send_sem=go_send.at[chunk, step], recv_sem=go_recv.at[chunk, source],
            device_id=place(target), device_id_type=MESH,
        )

    def back_copy(chunk, step, source, target):
        return pltpu.make_async_remote_copy(
            src_ref=back_box.at[:, share(chunk, target), :],
            dst_ref=field.at[:, share(chunk, source), :],
            send_sem=back_send.at[chunk, step], recv_sem=back_recv.at[chunk, source],
            device_id=place(target), device_id_type=MESH,
        )

    def start_all(copy, chunk):
        def start(step, _):
            copy(chunk, step, me, other(step)).start()
            return 0

        lax.fori_loop(1, devices, start, 0)

    def land_all(copy, chunk):
        def wait(step, _):
            copy(chunk, step, other(step), other(step)).wait_recv()
            return 0

        lax.fori_loop(1, devices, wait, 0)

    def drain_all(copy, chunk):
        def wait(step, _):
            copy(chunk, step, me, other(step)).wait_send()
            return 0

        lax.fori_loop(1, devices, wait, 0)

    for chunk, (first, end) in enumerate(chunks):
        rows = slice(2 * first * devices, 2 * end * devices)
        turned = three((xf_ref[0, rows, :], xf_ref[1, rows, :]), mixture, ((1,), (1,)))
        for t in range(tiles_out):
            send_box[t, rows, :] = turned[:, t * 128:(t + 1) * 128]
        start_all(go_copy, chunk)
        land_box[:, share(chunk, me), :] = send_box[:, share(chunk, me), :]

    for z in range(z_local):
        load(dens_hbm, dens, 1, z).wait()
        total = weights[0] * dens[0, z]
        for i in range(1, count):
            total = total + weights[i] * dens[i, z]
        out_ref[z * y_local:(z + 1) * y_local, :] = total
    total = weights[0] * (occ_ref[0] + block_mixing * occ_res_ref[0])
    for i in range(1, count):
        total = total + weights[i] * (occ_ref[i] + block_mixing * occ_res_ref[i])
    occ_out_ref[...] = mask * total
    lax.fori_loop(1, devices, drain_sum, 0)

    for copy in loads[1:]:
        copy.wait()
    z_forward = (zf_ref[0], zf_ref[1])
    z_back = (zb_ref[0], zb_ref[1])
    y_cosine = (yt_ref[0, 0], yt_ref[1, 0])
    y_sine = (yt_ref[0, 1], yt_ref[1, 1])
    shape = (2 * z_length, y_length)
    z_index = lax.rem(lax.broadcasted_iota(jnp.int32, shape, 0), z_length)
    y_index = lax.broadcasted_iota(jnp.int32, shape, 1)
    z_size = jnp.minimum(z_index, z_length - z_index).astype(jnp.float32)
    y_size = jnp.minimum(y_index, y_length - y_index).astype(jnp.float32)
    flat = z_size * z_size + y_size * y_size

    def filtered(wave, freq_x):
        size = freq_x.astype(jnp.float32)
        square = flat + size * size
        return split(wave * (square / (square + kerker_wave * kerker_wave)))

    for chunk, (first, end) in enumerate(chunks):
        size = 2 * (end - first)
        base = 2 * first * devices
        land_all(go_copy, chunk)
        for p in range(pencils):
            for f in range(size):
                joined = jnp.concatenate(
                    [
                        land_box[t, pl.ds(base + p * size + f, slabs, stride=pencils * size), :]
                        for t in range(tiles_out)
                    ],
                    axis=1,
                )
                for z in range(z_local):
                    planes[
                        2 * first + f, z * slabs:(z + 1) * slabs, p * y_local:(p + 1) * y_local
                    ] = joined[:, z * y_local:(z + 1) * y_local]
        block = split(planes[2 * first:2 * end].reshape(size * z_length, y_length))
        along_cosine = three(block, y_cosine, ((1,), (0,)))
        along_sine = three(block, y_sine, ((1,), (0,)))
        extra = first == 0
        for k in range(first, end):
            top, low = 2 * (k - first) * z_length, (2 * (k - first) + 1) * z_length
            stop = low + z_length
            real = along_cosine[top:low] + along_sine[low:stop]
            imag = along_cosine[low:stop] - along_sine[top:low]
            wave = three(z_forward, split(jnp.concatenate((real, imag), axis=0)), ((1,), (0,)))
            freq_x = me * slots_k + k
            spectrum[k - first] = three(z_back, filtered(wave, freq_x), ((1,), (0,)))
            if k == 0:
                freq_x = jnp.where(me == 0, x_length // 2, freq_x)
                spectrum[end] = three(z_back, filtered(wave, freq_x), ((1,), (0,)))
        used = end - first + (1 if extra else 0)
        block = split(spectrum[0:used].reshape(used * 2 * z_length, y_length))
        along_cosine = three(block, y_cosine, ((1,), (0,)))
        along_sine = three(block, y_sine, ((1,), (0,)))
        for k in range(first, end):
            top, low = 2 * (k - first) * z_length, (2 * (k - first) + 1) * z_length
            stop = low + z_length
            real = along_cosine[top:low] - along_sine[low:stop]
            if k == 0:
                top, low = 2 * end * z_length, (2 * end + 1) * z_length
                stop = low + z_length
            imag = along_cosine[low:stop] + along_sine[top:low]
            for c, part in enumerate((real, imag)):
                for p in range(pencils):
                    joined = jnp.concatenate(
                        [
                            part[z * slabs:(z + 1) * slabs, p * y_local:(p + 1) * y_local]
                            for z in range(z_local)
                        ],
                        axis=1,
                    )
                    start = base + p * size + 2 * (k - first) + c
                    for t in range(tiles_out):
                        back_box[t, pl.ds(start, slabs, stride=pencils * size), :] = joined[
                            :, t * 128:(t + 1) * 128
                        ]
        start_all(back_copy, chunk)
        field[:, share(chunk, me), :] = back_box[:, share(chunk, me), :]

    for chunk in range(len(chunks)):
        drain_all(go_copy, chunk)
    for chunk in range(len(chunks)):
        land_all(back_copy, chunk)
    for chunk in range(len(chunks)):
        drain_all(back_copy, chunk)


def finish_kernel(field_ref, dens_ref, occ_ref, xb_ref, out_ref, occ_out_ref):
    x_back = (xb_ref[0], xb_ref[1])
    occ_out_ref[...] = occ_ref[...]
    for t in range(field_ref.shape[0]):
        rows = slice(t * 128, (t + 1) * 128)
        out_ref[rows, :] = dens_ref[rows, :] + three(split(field_ref[t]), x_back, ((0,), (0,)))


def fused_body(
    density_history, residual_history, occupancy_history, occupancy_residual, species, slot_count
):
    count, z_local, y_local, x_length = residual_history.shape
    slabs = lax.axis_size("slab")
    pencils = lax.axis_size("pencil")
    devices = slabs * pencils
    z_length, y_length = z_local * slabs, y_local * pencils
    freqs = x_length // devices
    entry = np.arange(ORBITALS * ORBITALS)
    corner = np.maximum(entry // ORBITALS, entry % ORBITALS)[None].astype(np.int32)
    x_forward, x_back, *others = [
        jnp.asarray(t) for t in tables(x_length, y_length, z_length, pencils, slabs)
    ]
    constants = [x_forward, *others]
    chunks = len(cuts_of(freqs // 2))
    vmem = pl.BlockSpec(memory_space=pltpu.VMEM)
    smem = pl.BlockSpec(memory_space=pltpu.SMEM)
    hbm = pl.BlockSpec(memory_space=pltpu.HBM)
    box = (z_local * y_local // 128, devices * freqs, 128)
    sems = pltpu.SemaphoreType.DMA
    flat = jax.ShapeDtypeStruct((z_local * y_local, x_length), jnp.float32)
    blocks = jax.ShapeDtypeStruct(occupancy_history.shape[1:], jnp.float32)
    mixed, mixed_blocks, field = pl.pallas_call(
        functools.partial(
            mix_kernel, slabs, pencils,
            z_length * y_length * x_length, species.shape[0] * devices,
        ),
        out_shape=(flat, blocks, jax.ShapeDtypeStruct(box, jnp.float32)),
        in_specs=[hbm, hbm, vmem, vmem, smem, smem, vmem] + [hbm] * 4,
        out_specs=(vmem, vmem, vmem),
        scratch_shapes=[
            pltpu.VMEM(residual_history.shape, jnp.float32),
            pltpu.VMEM(residual_history.shape, jnp.float32),
            pltpu.VMEM((devices, 1, 128), jnp.float32),
            pltpu.VMEM(box, jnp.float32),
            pltpu.VMEM(box, jnp.float32),
            pltpu.VMEM((freqs, z_length, y_length), jnp.float32),
            pltpu.VMEM((freqs // 2 + 1, 2 * z_length, y_length), jnp.float32),
            pltpu.VMEM(box, jnp.float32),
            *[pltpu.VMEM(t.shape, t.dtype) for t in constants],
            sems((2, z_local)),
            sems((len(constants),)),
            sems((devices,)), sems((devices,)),
            sems((chunks, devices)), sems((chunks, devices)),
            sems((chunks, devices)), sems((chunks, devices)),
        ],
        compiler_params=pltpu.CompilerParams(
            collective_id=0, has_side_effects=True, vmem_limit_bytes=56000 * 1024
        ),
    )(
        residual_history, density_history, occupancy_history, occupancy_residual,
        species, slot_count, jnp.asarray(corner), *constants,
    )
    new_density, new_blocks = pl.pallas_call(
        finish_kernel,
        out_shape=(flat, blocks),
        in_specs=[vmem] * 4,
        out_specs=(vmem, vmem),
    )(field, mixed, mixed_blocks, x_back)
    return new_density.reshape(z_local, y_local, x_length), new_blocks


def solution(mesh):
    placed = (
        P(None, "slab", "pencil", None),
        P(None, "slab", "pencil", None),
        P(None, ("slab", "pencil"), None),
        P(None, ("slab", "pencil"), None),
        P(("slab", "pencil")),
        P(("slab", "pencil")),
    )
    devices = mesh.shape["slab"] * mesh.shape["pencil"]

    def chosen(*arrays):
        x_length = arrays[0].shape[3]
        _, z_local, y_local, _ = arrays[0].shape
        fits = (
            x_length % (2 * devices) == 0
            and mesh.shape["slab"] % 8 == 0
            and y_local % 16 == 0
            and z_local * y_local % 128 == 0
        )
        return (fused_body if fits else body)(*arrays)

    return jax.shard_map(
        chosen,
        mesh=mesh,
        in_specs=placed,
        out_specs=(P("slab", "pencil", None), P(("slab", "pencil"), None)),
        check_vma=False,
    )
```

profile of v0, /device:TPU:25, one launch (start us, length us, event | category | flops | bytes accessed | tf_op | source)
XLA Modules:
  0.0 62.1 jit_solution(9084574078738650459)
XLA Ops:
  1.3 57.1 %shard_map.131 = (f32[640,320]{1,0:T(8,128)}, f32[24,324]{1,0:T(8,128)}, f32[5,320,128]{2,1,0:T(8,128)}) custom-call(f32[7,8,80,320]{3,2,1,0:T(8,128)} %res_hbm.1, f32[7,8,80,320]{3,2,1,0:T(8,128)} %dens_hbm.1, f32[7,24,324]{2,1,0:T(8,128)} %occ_ref.1, f32[7,24,324]{2,1,0:T(8,128)} %occ_res_ref.1, s32[24]{0:T(128)} %species_ref.1, s32[1]{0:T(128)S(6)} %copy.14.live_ref, ...), custom_call_target="tpu_custom_call" | custom-call | tf_op jit(solution)/shard_map/pallas_call | solution.py:629
  58.4 3.7 %shard_map.132 = (f32[640,320]{1,0:T(8,128)}, f32[24,324]{1,0:T(8,128)}) custom-call(f32[5,320,128]{2,1,0:T(8,128)} %get-tuple-element.7.field_ref, f32[640,320]{1,0:T(8,128)} %get-tuple-element.8.dens_ref, f32[24,324]{1,0:T(8,128)} %get-tuple-element.9.occ_ref, bf16[2,320,320]{2,1,0:T(8,128)(2,1)} %constant.13.clone.xb_ref), custom_call_target="tpu_custom_call" | custom-call | tf_op jit(solution)/shard_map/pallas_call | solution.py:660
where the time goes:
time: 62.3 us; the launch traced here: 62.1 us
  Pallas kernels  60.8 us (98%)
  between operations  1.29 us (2%)
    pallas_call x1, Pallas kernels, fused_body(): pl.pallas_call(functools.partial(mix_kernel, slabs, pencils, z_length * y...  57.1 us
    pallas_call x1, Pallas kernels, fused_body(): pl.pallas_call(finish_kernel, out_shape=(flat, blocks), in_specs=[vmem] *...  3.73 us

commit v1 on v0

--- a/solution.py
+++ b/solution.py
@@ -216,6 +216,7 @@
 
 
 MESH = pl.DeviceIdType.MESH
+VMEM_LIMIT = 40000 * 1024
 
 
 def split(value):
@@ -310,12 +311,13 @@
 
 def mix_kernel(
     slabs, pencils, cells, slots,
-    res_hbm, dens_hbm, occ_ref, occ_res_ref, species_ref, live_ref, corner_ref,
-    xf_hbm, yt_hbm, zf_hbm, zb_hbm,
-    out_ref, occ_out_ref, field,
-    res, dens, sums, send_box, land_box, planes, spectrum, back_box,
-    xf_ref, yt_ref, zf_ref, zb_ref,
-    load_sem, table_sem, sum_send, sum_recv, go_send, go_recv, back_send, back_recv,
+    live_ref, res_hbm, dens_hbm, occ_hbm, occ_res_hbm, species_hbm, corner_hbm,
+    xf_hbm, yt_hbm, zf_hbm, zb_hbm, xb_hbm,
+    out_ref, occ_out_ref,
+    res, dens, occ_ref, occ_res_ref, species_ref, corner_ref,
+    first_turn, sums, send_box, land_box, planes, spectrum, back_box, field,
+    xf_ref, yt_ref, zf_ref, zb_ref, xb_ref,
+    res_sem, table_sem, sum_sem, go_send, go_recv, back_send, back_recv,
 ):
     devices = slabs * pencils
     count, z_local, y_local, x_length = res.shape
@@ -328,12 +330,33 @@
     pencil = lax.axis_index("pencil")
     me = slab * pencils + pencil
     pairs = pairs_of(count)
+    ends = cuts_of(slots_k)
+    chunks = list(zip([0] + ends[:-1], ends))
 
     def place(index):
         return (lax.div(index, pencils), lax.rem(index, pencils))
 
     def other(step):
         return lax.rem(me + step, devices)
+
+    sources = (
+        occ_res_hbm, species_hbm, corner_hbm, xf_hbm,
+        occ_hbm, dens_hbm, yt_hbm, zf_hbm, zb_hbm, xb_hbm,
+    )
+    targets = (
+        occ_res_ref, species_ref, corner_ref, xf_ref,
+        occ_ref, dens, yt_ref, zf_ref, zb_ref, xb_ref,
+    )
+    loads = [
+        pltpu.make_async_copy(a, b, table_sem.at[at])
+        for at, (a, b) in enumerate(zip(sources, targets))
+    ]
+    res_loads = [
+        pltpu.make_async_copy(res_hbm.at[:, z], res.at[:, z], res_sem.at[z])
+        for z in range(z_local)
+    ]
+    for copy in loads[:3] + res_loads + loads[3:4]:
+        copy.start()
 
     barrier = pltpu.get_barrier_semaphore()
 
@@ -345,150 +368,164 @@
 
     lax.fori_loop(1, devices, greet, 0)
 
-    def load(source, target, which, z):
-        return pltpu.make_async_copy(source.at[:, z], target.at[:, z], load_sem.at[which, z])
-
+    def wide(value):
+        width = value.shape[1]
+        if width == 128:
+            return value
+        return jnp.concatenate((value, jnp.zeros((8, 128 - width), value.dtype)), axis=1)
+
+    def lanes_of(length):
+        return [(at, min(at + 128, length)) for at in range(0, length, 128)]
+
+    for copy in loads[:3]:
+        copy.wait()
+    slot_count, entries = occ_ref.shape[1:]
+    species = species_ref[...]
+    orbitals = jnp.zeros_like(species)
+    for species_index, orbital_number in enumerate(species_orbitals):
+        orbitals = jnp.where(species == species_index, orbital_number, orbitals)
+    square = (slot_count, slot_count)
+    row_index = lax.broadcasted_iota(jnp.int32, square, 0)
+    column_index = lax.broadcasted_iota(jnp.int32, square, 1)
+    chosen = (row_index == column_index) & (column_index < live_ref[0])
+    limit = jnp.sum(
+        jnp.where(chosen, orbitals.astype(jnp.float32), 0.0), axis=1, keepdims=True
+    )
+    mask = (corner_ref[...] < limit).astype(jnp.float32)
+    ratio = cells / (100.0 * slots)
+    acc = [jnp.zeros((8, 128), jnp.float32) for _ in pairs]
+    for first in range(0, slot_count, 8):
+        for start, stop in lanes_of(entries):
+            part = [
+                wide(occ_res_ref[i, first:first + 8, start:stop] * mask[first:first + 8, start:stop])
+                for i in range(count)
+            ]
+            for at, (i, j) in enumerate(pairs):
+                acc[at] = acc[at] + part[i] * part[j]
+    acc = [value * ratio for value in acc]
     for z in range(z_local):
-        load(res_hbm, res, 0, z).start()
-    from_tables = (xf_hbm, yt_hbm, zf_hbm, zb_hbm)
-    to_tables = (xf_ref, yt_ref, zf_ref, zb_ref)
-    loads = [
-        pltpu.make_async_copy(a, b, table_sem.at[at])
-        for at, (a, b) in enumerate(zip(from_tables, to_tables))
-    ]
-    for copy in loads:
+        res_loads[z].wait()
+
+        def rows(step, acc):
+            acc = list(acc)
+            row = pl.multiple_of(step * 8, 8)
+            for start, stop in lanes_of(x_length):
+                part = [wide(res[i, z, pl.ds(row, 8), start:stop]) for i in range(count)]
+                for at, (i, j) in enumerate(pairs):
+                    acc[at] = acc[at] + part[i] * part[j]
+            return tuple(acc)
+
+        acc = lax.fori_loop(0, y_local // 8, rows, tuple(acc))
+    for copy in loads[4:]:
         copy.start()
-    for z in range(z_local):
-        load(dens_hbm, dens, 1, z).start()
-
-    limit_shape = (occ_ref.shape[1], 1)
-    slot_index = lax.broadcasted_iota(jnp.int32, limit_shape, 0)
-    limit = jnp.zeros(limit_shape, jnp.int32)
-    for slot in range(occ_ref.shape[1]):
-        orbitals = jnp.int32(0)
-        for species_index, orbital_number in enumerate(species_orbitals):
-            orbitals = jnp.where(species_ref[slot] == species_index, orbital_number, orbitals)
-        orbitals = jnp.where(slot < live_ref[0], orbitals, 0)
-        limit = jnp.where(slot_index == slot, orbitals, limit)
-    mask = (corner_ref[...] < limit).astype(jnp.float32)
-    blocks = [occ_res_ref[i] * mask for i in range(count)]
-    totals = [
-        jnp.sum(blocks[i] * blocks[j], keepdims=True) / (100.0 * slots) for i, j in pairs
-    ]
-    whole = x_length // 128
-    rest = x_length - whole * 128
-    for first, width, tiles in ((0, 128, whole), (whole * 128, rest, 1 if rest else 0)):
-        if tiles == 0:
-            continue
-        acc = [jnp.zeros((8, width), jnp.float32) for _ in pairs]
-        for z in range(z_local):
-            if first == 0:
-                load(res_hbm, res, 0, z).wait()
-
-            def rows(step, acc):
-                acc = list(acc)
-                row = pl.multiple_of(step * 8, 8)
-                for t in range(tiles):
-                    lane = first + 128 * t
-                    part = [res[i, z, pl.ds(row, 8), lane:lane + width] for i in range(count)]
-                    for at, (i, j) in enumerate(pairs):
-                        acc[at] = acc[at] + part[i] * part[j]
-                return tuple(acc)
-
-            acc = lax.fori_loop(0, y_local // 8, rows, tuple(acc))
-        totals = [t + jnp.sum(a, keepdims=True) / cells for t, a in zip(totals, acc)]
+    stacked = jnp.concatenate([jnp.sum(a, axis=0, keepdims=True) for a in acc], axis=0)
+    totals = jnp.sum(stacked, axis=1, keepdims=True) / cells
+    shape = (len(pairs), 128)
+    pair_index = lax.broadcasted_iota(jnp.int32, shape, 0)
+    across = lax.broadcasted_iota(jnp.int32, shape, 1)
+    packed = jnp.sum(jnp.where(pair_index == across, totals, 0.0), axis=0, keepdims=True)
+    sums[pl.ds(me, 1), :] = packed
+
+    pl.semaphore_wait(barrier, devices - 1)
+
+    def sum_copy(source, target):
+        return pltpu.make_async_remote_copy(
+            src_ref=sums.at[pl.ds(source, 1)], dst_ref=sums.at[pl.ds(source, 1)],
+            send_sem=sum_sem.at[0], recv_sem=sum_sem.at[1],
+            device_id=place(target), device_id_type=MESH,
+        )
+
+    def start_sum(step, _):
+        sum_copy(me, other(step)).start()
+        return 0
+
+    lax.fori_loop(1, devices, start_sum, 0)
+    all_sums = pltpu.make_async_remote_copy(
+        src_ref=sums.at[pl.ds(0, devices - 1)], dst_ref=sums.at[pl.ds(0, devices - 1)],
+        send_sem=sum_sem.at[0], recv_sem=sum_sem.at[1],
+        device_id=place(other(1)), device_id_type=MESH,
+    )
+
+    loads[3].wait()
+    opening = slice(0, 2 * ends[0] * devices)
+
+    def turn(i, _):
+        history = split(res[i].reshape(z_local * y_local, x_length))
+        left = (xf_ref[0, opening, :], xf_ref[1, opening, :])
+        first_turn[i] = three(left, history, ((1,), (1,)))
+        return 0
+
+    lax.fori_loop(0, count, turn, 0)
+
+    all_sums.wait_recv()
+    gathered = jnp.sum(sums[...], axis=0, keepdims=True)
     lane_index = lax.broadcasted_iota(jnp.int32, (1, 128), 1)
-    packed = jnp.zeros((1, 128), jnp.float32)
-    for at, value in enumerate(totals):
-        packed = jnp.where(lane_index == at, value, packed)
-    sums[me] = packed
-
-    pl.semaphore_wait(barrier, devices - 1)
-
-    def sum_copy(step, source):
-        return pltpu.make_async_remote_copy(
-            src_ref=sums.at[source], dst_ref=sums.at[source],
-            send_sem=sum_send.at[step], recv_sem=sum_recv.at[source],
-            device_id=place(other(step)), device_id_type=MESH,
-        )
-
-    def start_sum(step, _):
-        sum_copy(step, me).start()
-        return 0
-
-    def wait_sum(step, _):
-        sum_copy(step, other(step)).wait_recv()
-        return 0
-
-    def drain_sum(step, _):
-        sum_copy(step, me).wait_send()
-        return 0
-
-    lax.fori_loop(1, devices, start_sum, 0)
-    lax.fori_loop(1, devices, wait_sum, 0)
-    gathered = sums[0]
-    for d in range(1, devices):
-        gathered = gathered + sums[d]
     entry = {
         pair: jnp.sum(jnp.where(lane_index == at, gathered, 0.0), axis=1, keepdims=True)
         for at, pair in enumerate(pairs)
     }
     weights = solve_weights(entry, count)
 
-    loads[0].wait()
-    mixture = []
-    for z in range(z_local):
-        total = weights[0] * res[0, z]
-        for i in range(1, count):
-            total = total + weights[i] * res[i, z]
-        mixture.append(total)
-    mixture = split(jnp.concatenate(mixture, axis=0))
-    ends = cuts_of(slots_k)
-    chunks = list(zip([0] + ends[:-1], ends))
-
     def share(chunk, index):
         first, end = chunks[chunk]
         size = 2 * (end - first)
         return pl.ds(2 * first * devices + index * size, size)
 
-    def go_copy(chunk, step, source, target):
+    def go_copy(chunk, source, target):
         return pltpu.make_async_remote_copy(
             src_ref=send_box.at[:, share(chunk, target), :],
             dst_ref=land_box.at[:, share(chunk, source), :],
-            send_sem=go_send.at[chunk, step], recv_sem=go_recv.at[chunk, source],
+            send_sem=go_send.at[0], recv_sem=go_recv.at[chunk],
             device_id=place(target), device_id_type=MESH,
         )
 
-    def back_copy(chunk, step, source, target):
+    def back_copy(chunk, source, target):
         return pltpu.make_async_remote_copy(
             src_ref=back_box.at[:, share(chunk, target), :],
             dst_ref=field.at[:, share(chunk, source), :],
-            send_sem=back_send.at[chunk, step], recv_sem=back_recv.at[chunk, source],
+            send_sem=back_send.at[0], recv_sem=back_recv.at[chunk],
             device_id=place(target), device_id_type=MESH,
         )
 
     def start_all(copy, chunk):
         def start(step, _):
-            copy(chunk, step, me, other(step)).start()
+            copy(chunk, me, other(step)).start()
             return 0
 
         lax.fori_loop(1, devices, start, 0)
 
-    def land_all(copy, chunk):
-        def wait(step, _):
-            copy(chunk, step, other(step), other(step)).wait_recv()
-            return 0
-
-        lax.fori_loop(1, devices, wait, 0)
-
-    def drain_all(copy, chunk):
-        def wait(step, _):
-            copy(chunk, step, me, other(step)).wait_send()
-            return 0
-
-        lax.fori_loop(1, devices, wait, 0)
-
+    def whole(source, target, rows, send, recv):
+        return pltpu.make_async_remote_copy(
+            src_ref=source.at[:, rows, :], dst_ref=target.at[:, rows, :],
+            send_sem=send, recv_sem=recv, device_id=place(other(1)), device_id_type=MESH,
+        )
+
+    def land_all(source, target, send, recv, chunk):
+        first, end = chunks[chunk]
+        rows = pl.ds(2 * first * devices, 2 * (end - first) * (devices - 1))
+        whole(source, target, rows, send.at[0], recv.at[chunk]).wait_recv()
+
+    def drain_all(source, target, send, recv):
+        rows = pl.ds(0, freqs * (devices - 1))
+        whole(source, target, rows, send.at[0], recv.at[0]).wait_send()
+
+    def mixed(parts):
+        total = weights[0] * parts[0]
+        for i in range(1, count):
+            total = total + weights[i] * parts[i]
+        return total
+
+    turned = mixed([first_turn[i] for i in range(count)])
+    for t in range(tiles_out):
+        send_box[t, opening, :] = turned[:, t * 128:(t + 1) * 128]
+    start_all(go_copy, 0)
+    land_box[:, share(0, me), :] = send_box[:, share(0, me), :]
+
+    mixture = [mixed([res[i, z] for i in range(count)]) for z in range(z_local)]
+    mixture = split(jnp.concatenate(mixture, axis=0))
     for chunk, (first, end) in enumerate(chunks):
+        if chunk == 0:
+            continue
         rows = slice(2 * first * devices, 2 * end * devices)
         turned = three((xf_ref[0, rows, :], xf_ref[1, rows, :]), mixture, ((1,), (1,)))
         for t in range(tiles_out):
@@ -496,20 +533,15 @@
         start_all(go_copy, chunk)
         land_box[:, share(chunk, me), :] = send_box[:, share(chunk, me), :]
 
+    for copy in loads[4:]:
+        copy.wait()
     for z in range(z_local):
-        load(dens_hbm, dens, 1, z).wait()
-        total = weights[0] * dens[0, z]
-        for i in range(1, count):
-            total = total + weights[i] * dens[i, z]
-        out_ref[z * y_local:(z + 1) * y_local, :] = total
-    total = weights[0] * (occ_ref[0] + block_mixing * occ_res_ref[0])
-    for i in range(1, count):
-        total = total + weights[i] * (occ_ref[i] + block_mixing * occ_res_ref[i])
-    occ_out_ref[...] = mask * total
-    lax.fori_loop(1, devices, drain_sum, 0)
-
-    for copy in loads[1:]:
-        copy.wait()
+        out_ref[z * y_local:(z + 1) * y_local, :] = mixed([dens[i, z] for i in range(count)])
+    occ_out_ref[...] = mask * mixed(
+        [occ_ref[i] + block_mixing * occ_res_ref[i] for i in range(count)]
+    )
+    all_sums.wait_send()
+
     z_forward = (zf_ref[0], zf_ref[1])
     z_back = (zb_ref[0], zb_ref[1])
     y_cosine = (yt_ref[0, 0], yt_ref[1, 0])
@@ -529,7 +561,7 @@
     for chunk, (first, end) in enumerate(chunks):
         size = 2 * (end - first)
         base = 2 * first * devices
-        land_all(go_copy, chunk)
+        land_all(send_box, land_box, go_send, go_recv, chunk)
         for p in range(pencils):
             for f in range(size):
                 joined = jnp.concatenate(
@@ -587,20 +619,17 @@
         start_all(back_copy, chunk)
         field[:, share(chunk, me), :] = back_box[:, share(chunk, me), :]
 
-    for chunk in range(len(chunks)):
-        drain_all(go_copy, chunk)
-    for chunk in range(len(chunks)):
-        land_all(back_copy, chunk)
-    for chunk in range(len(chunks)):
-        drain_all(back_copy, chunk)
-
-
-def finish_kernel(field_ref, dens_ref, occ_ref, xb_ref, out_ref, occ_out_ref):
-    x_back = (xb_ref[0], xb_ref[1])
-    occ_out_ref[...] = occ_ref[...]
-    for t in range(field_ref.shape[0]):
-        rows = slice(t * 128, (t + 1) * 128)
-        out_ref[rows, :] = dens_ref[rows, :] + three(split(field_ref[t]), x_back, ((0,), (0,)))
+    drain_all(send_box, land_box, go_send, go_recv)
+    for chunk, (first, end) in enumerate(chunks):
+        land_all(back_box, field, back_send, back_recv, chunk)
+        used = slice(2 * first * devices, 2 * end * devices)
+        table = (xb_ref[0, used, :], xb_ref[1, used, :])
+        for t in range(tiles_out):
+            rows = slice(t * 128, (t + 1) * 128)
+            out_ref[rows, :] = out_ref[rows, :] + three(
+                split(field[t, used, :]), table, ((0,), (0,))
+            )
+    drain_all(back_box, field, back_send, back_recv)
 
 
 def fused_body(
@@ -613,56 +642,56 @@
     z_length, y_length = z_local * slabs, y_local * pencils
     freqs = x_length // devices
     entry = np.arange(ORBITALS * ORBITALS)
-    corner = np.maximum(entry // ORBITALS, entry % ORBITALS)[None].astype(np.int32)
+    corner = np.maximum(entry // ORBITALS, entry % ORBITALS)[None].astype(np.float32)
     x_forward, x_back, *others = [
         jnp.asarray(t) for t in tables(x_length, y_length, z_length, pencils, slabs)
     ]
-    constants = [x_forward, *others]
-    chunks = len(cuts_of(freqs // 2))
+    constants = [x_forward, *others, x_back]
+    ends = cuts_of(freqs // 2)
+    chunks = len(ends)
     vmem = pl.BlockSpec(memory_space=pltpu.VMEM)
-    smem = pl.BlockSpec(memory_space=pltpu.SMEM)
     hbm = pl.BlockSpec(memory_space=pltpu.HBM)
     box = (z_local * y_local // 128, devices * freqs, 128)
     sems = pltpu.SemaphoreType.DMA
     flat = jax.ShapeDtypeStruct((z_local * y_local, x_length), jnp.float32)
     blocks = jax.ShapeDtypeStruct(occupancy_history.shape[1:], jnp.float32)
-    mixed, mixed_blocks, field = pl.pallas_call(
+    smalls = [
+        occupancy_history, occupancy_residual, species[None], jnp.asarray(corner)
+    ]
+    new_density, new_blocks = pl.pallas_call(
         functools.partial(
             mix_kernel, slabs, pencils,
             z_length * y_length * x_length, species.shape[0] * devices,
         ),
-        out_shape=(flat, blocks, jax.ShapeDtypeStruct(box, jnp.float32)),
-        in_specs=[hbm, hbm, vmem, vmem, smem, smem, vmem] + [hbm] * 4,
-        out_specs=(vmem, vmem, vmem),
+        out_shape=(flat, blocks),
+        in_specs=[pl.BlockSpec(memory_space=pltpu.SMEM)] + [hbm] * (6 + len(constants)),
+        out_specs=(vmem, vmem),
         scratch_shapes=[
             pltpu.VMEM(residual_history.shape, jnp.float32),
             pltpu.VMEM(residual_history.shape, jnp.float32),
-            pltpu.VMEM((devices, 1, 128), jnp.float32),
+            *[pltpu.VMEM(t.shape, t.dtype) for t in smalls],
+            pltpu.VMEM((count, 2 * ends[0] * devices, z_local * y_local), jnp.float32),
+            pltpu.VMEM((devices, 128), jnp.float32),
             pltpu.VMEM(box, jnp.float32),
             pltpu.VMEM(box, jnp.float32),
             pltpu.VMEM((freqs, z_length, y_length), jnp.float32),
             pltpu.VMEM((freqs // 2 + 1, 2 * z_length, y_length), jnp.float32),
             pltpu.VMEM(box, jnp.float32),
+            pltpu.VMEM(box, jnp.float32),
             *[pltpu.VMEM(t.shape, t.dtype) for t in constants],
-            sems((2, z_local)),
-            sems((len(constants),)),
-            sems((devices,)), sems((devices,)),
-            sems((chunks, devices)), sems((chunks, devices)),
-            sems((chunks, devices)), sems((chunks, devices)),
+            sems((z_local,)),
+            sems((5 + len(constants),)),
+            sems((2,)),
+            sems((1,)), sems((chunks,)),
+            sems((1,)), sems((chunks,)),
         ],
         compiler_params=pltpu.CompilerParams(
-            collective_id=0, has_side_effects=True, vmem_limit_bytes=56000 * 1024
+            collective_id=0, has_side_effects=True, vmem_limit_bytes=VMEM_LIMIT
         ),
-    )(
-        residual_history, density_history, occupancy_history, occupancy_residual,
-        species, slot_count, jnp.asarray(corner), *constants,
-    )
-    new_density, new_blocks = pl.pallas_call(
-        finish_kernel,
-        out_shape=(flat, blocks),
-        in_specs=[vmem] * 4,
-        out_specs=(vmem, vmem),
-    )(field, mixed, mixed_blocks, x_back)
+    )(slot_count, *[
+        pltpu.with_memory_space_constraint(value, pltpu.HBM)
+        for value in (residual_history, density_history, *smalls, *constants)
+    ])
     return new_density.reshape(z_local, y_local, x_length), new_blocks
 
 

time: 62.3 us -> 52.9 us (0.85)
  Pallas kernels: 60.8 us -> 49.5 us
  local copies, waits for them, and re-layouts: 0 us -> 1.56 us
    pallas_call x1, Pallas kernels: 57.1 us -> 49.5 us  [fused_body(): pl.pallas_call(functools.partial(mix_kernel, slabs, pencils, z_length * y...]
    pallas_call x1 -> x0, Pallas kernels: 3.73 us -> none  [fused_body(): pl.pallas_call(finish_kernel, out_shape=(flat, blocks), in_specs=[vmem] *...]
    unnamed x0 -> x2, local copies, waits for them, and re-layouts: none -> 1.56 us
where the time goes in v1:
time: 52.9 us; the launch traced here: 52.4 us
  Pallas kernels  49.5 us (94%)
  local copies, waits for them, and re-layouts  1.56 us (3%)
  between operations  1.29 us (2%)
    pallas_call x1, Pallas kernels, fused_body(): pl.pallas_call(functools.partial(mix_kernel, slabs, pencils, z_length * y...  49.5 us
    unnamed x2, local copies, waits for them, and re-layouts  1.56 us

profile of v1, /device:TPU:25, one launch (start us, length us, event | category | flops | bytes accessed | tf_op | source)
XLA Modules:
  0.0 52.4 jit_solution(10588192000557900672)
XLA Ops:
  1.3 49.5 %shard_map.131 = (f32[640,320]{1,0:T(8,128)S(1)}, f32[24,324]{1,0:T(8,128)S(1)}) custom-call(s32[1]{0:T(128)S(6)} %copy.16.live_ref, f32[7,8,80,320]{3,2,1,0:T(8,128)} %res_hbm.1, f32[7,8,80,320]{3,2,1,0:T(8,128)} %dens_hbm.1, f32[7,24,324]{2,1,0:T(8,128)} %occ_hbm.1, f32[7,24,324]{2,1,0:T(8,128)} %occ_res_hbm.1, s32[1,24]{1,0:T(1,128)} %bitcast.3, ...), custom_call_target="tpu_custom_call" | custom-call | tf_op jit(solution)/shard_map/pallas_call | solution.py:661
  50.8 0.9 %copy.17 = f32[8,80,320]{2,1,0:T(8,128)} copy(f32[8,80,320]{2,1,0:T(8,128)S(1)} %bitcast.2) | data formatting | bytes 1638400
  51.7 0.6 %copy.18 = f32[24,324]{1,0:T(8,128)} copy(f32[24,324]{1,0:T(8,128)S(1)} %get-tuple-element.9) | data formatting | bytes 62208

commit v2 on v1

--- a/solution.py
+++ b/solution.py
@@ -313,7 +313,7 @@
     slabs, pencils, cells, slots,
     live_ref, res_hbm, dens_hbm, occ_hbm, occ_res_hbm, species_hbm, corner_hbm,
     xf_hbm, yt_hbm, zf_hbm, zb_hbm, xb_hbm,
-    out_ref, occ_out_ref,
+    out_ref, occ_out_ref, last,
     res, dens, occ_ref, occ_res_ref, species_ref, corner_ref,
     first_turn, sums, send_box, land_box, planes, spectrum, back_box, field,
     xf_ref, yt_ref, zf_ref, zb_ref, xb_ref,
@@ -351,11 +351,12 @@
         pltpu.make_async_copy(a, b, table_sem.at[at])
         for at, (a, b) in enumerate(zip(sources, targets))
     ]
-    res_loads = [
-        pltpu.make_async_copy(res_hbm.at[:, z], res.at[:, z], res_sem.at[z])
-        for z in range(z_local)
-    ]
-    for copy in loads[:3] + res_loads + loads[3:4]:
+
+    def res_load(z):
+        return pltpu.make_async_copy(res_hbm.at[:, z], res.at[:, z], res_sem.at[z])
+
+    res_loads = [res_load(z) for z in range(z_local)]
+    for copy in loads[1:3] + res_loads + loads[:1] + loads[3:4]:
         copy.start()
 
     barrier = pltpu.get_barrier_semaphore()
@@ -376,6 +377,19 @@
 
     def lanes_of(length):
         return [(at, min(at + 128, length)) for at in range(0, length, 128)]
+
+    def plane(z, acc):
+        acc = list(acc)
+        res_load(z).wait()
+        for row in range(0, y_local, 8):
+            for start, stop in lanes_of(x_length):
+                part = [wide(res[i, z, row:row + 8, start:stop]) for i in range(count)]
+                for at, (i, j) in enumerate(pairs):
+                    acc[at] = acc[at] + part[i] * part[j]
+        return tuple(acc)
+
+    nothing = tuple(jnp.zeros((8, 128), jnp.float32) for _ in pairs)
+    acc = lax.fori_loop(0, z_local, plane, nothing)
 
     for copy in loads[:3]:
         copy.wait()
@@ -393,7 +407,7 @@
     )
     mask = (corner_ref[...] < limit).astype(jnp.float32)
     ratio = cells / (100.0 * slots)
-    acc = [jnp.zeros((8, 128), jnp.float32) for _ in pairs]
+    blocks_acc = [jnp.zeros((8, 128), jnp.float32) for _ in pairs]
     for first in range(0, slot_count, 8):
         for start, stop in lanes_of(entries):
             part = [
@@ -401,21 +415,8 @@
                 for i in range(count)
             ]
             for at, (i, j) in enumerate(pairs):
-                acc[at] = acc[at] + part[i] * part[j]
-    acc = [value * ratio for value in acc]
-    for z in range(z_local):
-        res_loads[z].wait()
-
-        def rows(step, acc):
-            acc = list(acc)
-            row = pl.multiple_of(step * 8, 8)
-            for start, stop in lanes_of(x_length):
-                part = [wide(res[i, z, pl.ds(row, 8), start:stop]) for i in range(count)]
-                for at, (i, j) in enumerate(pairs):
-                    acc[at] = acc[at] + part[i] * part[j]
-            return tuple(acc)
-
-        acc = lax.fori_loop(0, y_local // 8, rows, tuple(acc))
+                blocks_acc[at] = blocks_acc[at] + part[i] * part[j]
+    acc = [value + blocks * ratio for value, blocks in zip(acc, blocks_acc)]
     for copy in loads[4:]:
         copy.start()
     stacked = jnp.concatenate([jnp.sum(a, axis=0, keepdims=True) for a in acc], axis=0)
@@ -449,13 +450,10 @@
     loads[3].wait()
     opening = slice(0, 2 * ends[0] * devices)
 
-    def turn(i, _):
+    left = (xf_ref[0, opening, :], xf_ref[1, opening, :])
+    for i in range(count):
         history = split(res[i].reshape(z_local * y_local, x_length))
-        left = (xf_ref[0, opening, :], xf_ref[1, opening, :])
         first_turn[i] = three(left, history, ((1,), (1,)))
-        return 0
-
-    lax.fori_loop(0, count, turn, 0)
 
     all_sums.wait_recv()
     gathered = jnp.sum(sums[...], axis=0, keepdims=True)
@@ -479,10 +477,15 @@
             device_id=place(target), device_id_type=MESH,
         )
 
+    def landing(chunk, rows):
+        if chunk < len(chunks) - 1:
+            return field.at[:, rows, :]
+        return last.at[:, pl.ds(rows.start - 2 * chunks[chunk][0] * devices, rows.size), :]
+
     def back_copy(chunk, source, target):
         return pltpu.make_async_remote_copy(
             src_ref=back_box.at[:, share(chunk, target), :],
-            dst_ref=field.at[:, share(chunk, source), :],
+            dst_ref=landing(chunk, share(chunk, source)),
             send_sem=back_send.at[0], recv_sem=back_recv.at[chunk],
             device_id=place(target), device_id_type=MESH,
         )
@@ -617,11 +620,18 @@
                             :, t * 128:(t + 1) * 128
                         ]
         start_all(back_copy, chunk)
-        field[:, share(chunk, me), :] = back_box[:, share(chunk, me), :]
+        landing(chunk, share(chunk, me))[...] = back_box[:, share(chunk, me), :]
 
     drain_all(send_box, land_box, go_send, go_recv)
     for chunk, (first, end) in enumerate(chunks):
-        land_all(back_box, field, back_send, back_recv, chunk)
+        rows = pl.ds(2 * first * devices, 2 * (end - first) * (devices - 1))
+        pltpu.make_async_remote_copy(
+            src_ref=back_box.at[:, rows, :], dst_ref=landing(chunk, rows),
+            send_sem=back_send.at[0], recv_sem=back_recv.at[chunk],
+            device_id=place(other(1)), device_id_type=MESH,
+        ).wait_recv()
+        if chunk == len(chunks) - 1:
+            continue
         used = slice(2 * first * devices, 2 * end * devices)
         table = (xb_ref[0, used, :], xb_ref[1, used, :])
         for t in range(tiles_out):
@@ -629,7 +639,21 @@
             out_ref[rows, :] = out_ref[rows, :] + three(
                 split(field[t, used, :]), table, ((0,), (0,))
             )
-    drain_all(back_box, field, back_send, back_recv)
+    drain_all(back_box, back_box, back_send, back_recv)
+
+
+def finish_kernel(last, dens_ref, occ_ref, xb_ref, out_hbm, occ_hbm, out_ref, sem):
+    tiles = last.shape[0]
+    table = (xb_ref[0], xb_ref[1])
+    copies = [pltpu.make_async_copy(occ_ref, occ_hbm, sem.at[tiles])]
+    copies[0].start()
+    for t in range(tiles):
+        rows = slice(t * 128, (t + 1) * 128)
+        out_ref[rows, :] = dens_ref[rows, :] + three(split(last[t]), table, ((0,), (0,)))
+        copies.append(pltpu.make_async_copy(out_ref.at[rows], out_hbm.at[rows], sem.at[t]))
+        copies[-1].start()
+    for copy in copies:
+        copy.wait()
 
 
 def fused_body(
@@ -643,12 +667,13 @@
     freqs = x_length // devices
     entry = np.arange(ORBITALS * ORBITALS)
     corner = np.maximum(entry // ORBITALS, entry % ORBITALS)[None].astype(np.float32)
-    x_forward, x_back, *others = [
-        jnp.asarray(t) for t in tables(x_length, y_length, z_length, pencils, slabs)
-    ]
+    x_forward, x_back, *others = tables(x_length, y_length, z_length, pencils, slabs)
     constants = [x_forward, *others, x_back]
     ends = cuts_of(freqs // 2)
     chunks = len(ends)
+    late = 2 * ends[-2] * devices if chunks > 1 else 0
+    constants[-1] = x_back[:, :late] if late else x_back[:, :16]
+    constants = [jnp.asarray(t) for t in constants]
     vmem = pl.BlockSpec(memory_space=pltpu.VMEM)
     hbm = pl.BlockSpec(memory_space=pltpu.HBM)
     box = (z_local * y_local // 128, devices * freqs, 128)
@@ -658,14 +683,14 @@
     smalls = [
         occupancy_history, occupancy_residual, species[None], jnp.asarray(corner)
     ]
-    new_density, new_blocks = pl.pallas_call(
+    mixed, mixed_blocks, last = pl.pallas_call(
         functools.partial(
             mix_kernel, slabs, pencils,
             z_length * y_length * x_length, species.shape[0] * devices,
         ),
-        out_shape=(flat, blocks),
+        out_shape=(flat, blocks, jax.ShapeDtypeStruct((box[0], box[1] - late, 128), jnp.float32)),
         in_specs=[pl.BlockSpec(memory_space=pltpu.SMEM)] + [hbm] * (6 + len(constants)),
-        out_specs=(vmem, vmem),
+        out_specs=(vmem, vmem, vmem),
         scratch_shapes=[
             pltpu.VMEM(residual_history.shape, jnp.float32),
             pltpu.VMEM(residual_history.shape, jnp.float32),
@@ -677,7 +702,7 @@
             pltpu.VMEM((freqs, z_length, y_length), jnp.float32),
             pltpu.VMEM((freqs // 2 + 1, 2 * z_length, y_length), jnp.float32),
             pltpu.VMEM(box, jnp.float32),
-            pltpu.VMEM(box, jnp.float32),
+            pltpu.VMEM((box[0], late or 16, 128), jnp.float32),
             *[pltpu.VMEM(t.shape, t.dtype) for t in constants],
             sems((z_local,)),
             sems((5 + len(constants),)),
@@ -692,6 +717,15 @@
         pltpu.with_memory_space_constraint(value, pltpu.HBM)
         for value in (residual_history, density_history, *smalls, *constants)
     ])
+    tiles = box[0]
+    new_density, new_blocks = pl.pallas_call(
+        finish_kernel,
+        out_shape=(flat, blocks),
+        in_specs=[vmem] * 4,
+        out_specs=(hbm, hbm),
+        scratch_shapes=[pltpu.VMEM(flat.shape, flat.dtype), sems((tiles + 1,))],
+        compiler_params=pltpu.CompilerParams(vmem_limit_bytes=8 * 1024 * 1024),
+    )(last, mixed, mixed_blocks, jnp.asarray(x_back[:, late:]))
     return new_density.reshape(z_local, y_local, x_length), new_blocks
 
 

time: 52.9 us -> 49.8 us (0.941)
  local copies, waits for them, and re-layouts: 1.56 us -> 0.01 us
  Pallas kernels: 49.5 us -> 48.3 us
    pallas_call x1, Pallas kernels: 49.5 us -> 46.9 us  [fused_body(): pl.pallas_call(functools.partial(mix_kernel, slabs, pencils, z_length * y...]
    unnamed x2, local copies, waits for them, and re-layouts: 1.56 us -> 0.01 us
    pallas_call x0 -> x1, Pallas kernels: none -> 1.38 us  [fused_body(): pl.pallas_call(finish_kernel, out_shape=(flat, blocks), in_specs=[vmem] *...]
where the time goes in v2:
time: 49.8 us; the launch traced here: 49.6 us
  Pallas kernels  48.3 us (97%)
  between operations  1.3 us (3%)
    pallas_call x1, Pallas kernels, fused_body(): pl.pallas_call(functools.partial(mix_kernel, slabs, pencils, z_length * y...  46.9 us
    pallas_call x1, Pallas kernels, fused_body(): pl.pallas_call(finish_kernel, out_shape=(flat, blocks), in_specs=[vmem] *...  1.38 us

profile of v2, /device:TPU:25, one launch (start us, length us, event | category | flops | bytes accessed | tf_op | source)
XLA Modules:
  0.0 49.6 jit_solution(258995765162797215)
XLA Ops:
  1.3 0.0 copy-start
  1.3 46.9 %shard_map.140 = (f32[640,320]{1,0:T(8,128)S(1)}, f32[24,324]{1,0:T(8,128)S(1)}, f32[5,128,128]{2,1,0:T(8,128)S(1)}) custom-call(s32[1]{0:T(128)S(6)} %copy.15.live_ref, f32[7,8,80,320]{3,2,1,0:T(8,128)} %res_hbm.1, f32[7,8,80,320]{3,2,1,0:T(8,128)} %dens_hbm.1, f32[7,24,324]{2,1,0:T(8,128)} %occ_hbm.1, f32[7,24,324]{2,1,0:T(8,128)} %occ_res_hbm.1, ...), custom_call_target="tpu_custom_call" | custom-call | tf_op jit(solution)/shard_map/pallas_call | solution.py:686
  48.2 0.0 copy-done
  48.3 1.4 %shard_map.141 = (f32[640,320]{1,0:T(8,128)}, f32[24,324]{1,0:T(8,128)}) custom-call(f32[5,128,128]{2,1,0:T(8,128)S(1)} %get-tuple-element.7.last, f32[640,320]{1,0:T(8,128)S(1)} %get-tuple-element.8.dens_ref, f32[24,324]{1,0:T(8,128)S(1)} %get-tuple-element.9.occ_ref, bf16[2,128,320]{2,1,0:T(8,128)(2,1)S(1)} %copy-done), custom_call_target="tpu_custom_call" | custom-call | tf_op jit(solution)/shard_map/pallas_call | solution.py:721
Async XLA Ops:
  1.3 47.0 %copy-start = (bf16[2,128,320]{2,1,0:T(8,128)(2,1)S(1)}, bf16[2,128,320]{2,1,0:T(8,128)(2,1)}, u32[]{:S(2)}) copy-start(bf16[2,128,320]{2,1,0:T(8,128)(2,1)} %constant.20.clone.xb_ref) | copy-start | bytes 491524

commit v3 on v2

--- a/solution.py
+++ b/solution.py
@@ -333,11 +333,12 @@
     ends = cuts_of(slots_k)
     chunks = list(zip([0] + ends[:-1], ends))
 
-    def place(index):
-        return (lax.div(index, pencils), lax.rem(index, pencils))
-
-    def other(step):
-        return lax.rem(me + step, devices)
+    partners = []
+    for step in range(1, devices):
+        across = pencil + step % pencils
+        row = lax.rem(slab + step // pencils + lax.div(across, pencils), slabs)
+        column = lax.rem(across, pencils)
+        partners.append(((row, column), row * pencils + column))
 
     sources = (
         occ_res_hbm, species_hbm, corner_hbm, xf_hbm,
@@ -356,18 +357,13 @@
         return pltpu.make_async_copy(res_hbm.at[:, z], res.at[:, z], res_sem.at[z])
 
     res_loads = [res_load(z) for z in range(z_local)]
-    for copy in loads[1:3] + res_loads + loads[:1] + loads[3:4]:
+    for copy in loads[1:3] + res_loads[:-1] + loads[:1] + res_loads[-1:] + loads[3:4]:
         copy.start()
 
     barrier = pltpu.get_barrier_semaphore()
 
-    def greet(step, _):
-        pl.semaphore_signal(
-            barrier, inc=1, device_id=place(other(step)), device_id_type=MESH
-        )
-        return 0
-
-    lax.fori_loop(1, devices, greet, 0)
+    for spot, _ in partners:
+        pl.semaphore_signal(barrier, inc=1, device_id=spot, device_id_type=MESH)
 
     def wide(value):
         width = value.shape[1]
@@ -389,8 +385,7 @@
         return tuple(acc)
 
     nothing = tuple(jnp.zeros((8, 128), jnp.float32) for _ in pairs)
-    acc = lax.fori_loop(0, z_local, plane, nothing)
-
+    acc = lax.fori_loop(0, z_local - 1, plane, nothing)
     for copy in loads[:3]:
         copy.wait()
     slot_count, entries = occ_ref.shape[1:]
@@ -417,6 +412,8 @@
             for at, (i, j) in enumerate(pairs):
                 blocks_acc[at] = blocks_acc[at] + part[i] * part[j]
     acc = [value + blocks * ratio for value, blocks in zip(acc, blocks_acc)]
+    acc = plane(z_local - 1, acc)
+
     for copy in loads[4:]:
         copy.start()
     stacked = jnp.concatenate([jnp.sum(a, axis=0, keepdims=True) for a in acc], axis=0)
@@ -429,22 +426,16 @@
 
     pl.semaphore_wait(barrier, devices - 1)
 
-    def sum_copy(source, target):
-        return pltpu.make_async_remote_copy(
-            src_ref=sums.at[pl.ds(source, 1)], dst_ref=sums.at[pl.ds(source, 1)],
+    for spot, _ in partners:
+        pltpu.make_async_remote_copy(
+            src_ref=sums.at[pl.ds(me, 1)], dst_ref=sums.at[pl.ds(me, 1)],
             send_sem=sum_sem.at[0], recv_sem=sum_sem.at[1],
-            device_id=place(target), device_id_type=MESH,
-        )
-
-    def start_sum(step, _):
-        sum_copy(me, other(step)).start()
-        return 0
-
-    lax.fori_loop(1, devices, start_sum, 0)
+            device_id=spot, device_id_type=MESH,
+        ).start()
     all_sums = pltpu.make_async_remote_copy(
         src_ref=sums.at[pl.ds(0, devices - 1)], dst_ref=sums.at[pl.ds(0, devices - 1)],
         send_sem=sum_sem.at[0], recv_sem=sum_sem.at[1],
-        device_id=place(other(1)), device_id_type=MESH,
+        device_id=partners[0][0], device_id_type=MESH,
     )
 
     loads[3].wait()
@@ -469,12 +460,12 @@
         size = 2 * (end - first)
         return pl.ds(2 * first * devices + index * size, size)
 
-    def go_copy(chunk, source, target):
+    def go_copy(chunk, spot, target):
         return pltpu.make_async_remote_copy(
             src_ref=send_box.at[:, share(chunk, target), :],
-            dst_ref=land_box.at[:, share(chunk, source), :],
+            dst_ref=land_box.at[:, share(chunk, me), :],
             send_sem=go_send.at[0], recv_sem=go_recv.at[chunk],
-            device_id=place(target), device_id_type=MESH,
+            device_id=spot, device_id_type=MESH,
         )
 
     def landing(chunk, rows):
@@ -482,25 +473,22 @@
             return field.at[:, rows, :]
         return last.at[:, pl.ds(rows.start - 2 * chunks[chunk][0] * devices, rows.size), :]
 
-    def back_copy(chunk, source, target):
+    def back_copy(chunk, spot, target):
         return pltpu.make_async_remote_copy(
             src_ref=back_box.at[:, share(chunk, target), :],
-            dst_ref=landing(chunk, share(chunk, source)),
+            dst_ref=landing(chunk, share(chunk, me)),
             send_sem=back_send.at[0], recv_sem=back_recv.at[chunk],
-            device_id=place(target), device_id_type=MESH,
+            device_id=spot, device_id_type=MESH,
         )
 
     def start_all(copy, chunk):
-        def start(step, _):
-            copy(chunk, me, other(step)).start()
-            return 0
-
-        lax.fori_loop(1, devices, start, 0)
+        for spot, target in partners:
+            copy(chunk, spot, target).start()
 
     def whole(source, target, rows, send, recv):
         return pltpu.make_async_remote_copy(
             src_ref=source.at[:, rows, :], dst_ref=target.at[:, rows, :],
-            send_sem=send, recv_sem=recv, device_id=place(other(1)), device_id_type=MESH,
+            send_sem=send, recv_sem=recv, device_id=partners[0][0], device_id_type=MESH,
         )
 
     def land_all(source, target, send, recv, chunk):
@@ -628,7 +616,7 @@
         pltpu.make_async_remote_copy(
             src_ref=back_box.at[:, rows, :], dst_ref=landing(chunk, rows),
             send_sem=back_send.at[0], recv_sem=back_recv.at[chunk],
-            device_id=place(other(1)), device_id_type=MESH,
+            device_id=partners[0][0], device_id_type=MESH,
         ).wait_recv()
         if chunk == len(chunks) - 1:
             continue

time: 49.8 us -> 49.6 us (level)
  no operation moved by 1% of the time
where the time goes in v3:
time: 49.6 us; the launch traced here: 49.4 us
  Pallas kernels  48.1 us (97%)
  between operations  1.3 us (3%)
    pallas_call x1, Pallas kernels, fused_body(): pl.pallas_call(functools.partial(mix_kernel, slabs, pencils, z_length * y...  46.7 us
    pallas_call x1, Pallas kernels, fused_body(): pl.pallas_call(finish_kernel, out_shape=(flat, blocks), in_specs=[vmem] *...  1.4 us

profile of v3, /device:TPU:25, one launch (start us, length us, event | category | flops | bytes accessed | tf_op | source)
XLA Modules:
  0.0 49.4 jit_solution(2284792365954983049)
XLA Ops:
  1.3 0.0 copy-start
  1.3 46.7 %shard_map.140 = (f32[640,320]{1,0:T(8,128)S(1)}, f32[24,324]{1,0:T(8,128)S(1)}, f32[5,128,128]{2,1,0:T(8,128)S(1)}) custom-call(s32[1]{0:T(128)S(6)} %copy.15.live_ref, f32[7,8,80,320]{3,2,1,0:T(8,128)} %res_hbm.1, f32[7,8,80,320]{3,2,1,0:T(8,128)} %dens_hbm.1, f32[7,24,324]{2,1,0:T(8,128)} %occ_hbm.1, f32[7,24,324]{2,1,0:T(8,128)} %occ_res_hbm.1, ...), custom_call_target="tpu_custom_call" | custom-call | tf_op jit(solution)/shard_map/pallas_call | solution.py:674
  48.0 0.0 copy-done
  48.0 1.4 %shard_map.141 = (f32[640,320]{1,0:T(8,128)}, f32[24,324]{1,0:T(8,128)}) custom-call(f32[5,128,128]{2,1,0:T(8,128)S(1)} %get-tuple-element.7.last, f32[640,320]{1,0:T(8,128)S(1)} %get-tuple-element.8.dens_ref, f32[24,324]{1,0:T(8,128)S(1)} %get-tuple-element.9.occ_ref, bf16[2,128,320]{2,1,0:T(8,128)(2,1)S(1)} %copy-done), custom_call_target="tpu_custom_call" | custom-call | tf_op jit(solution)/shard_map/pallas_call | solution.py:709
Async XLA Ops:
  1.3 46.7 %copy-start = (bf16[2,128,320]{2,1,0:T(8,128)(2,1)S(1)}, bf16[2,128,320]{2,1,0:T(8,128)(2,1)}, u32[]{:S(2)}) copy-start(bf16[2,128,320]{2,1,0:T(8,128)(2,1)} %constant.20.clone.xb_ref) | copy-start | bytes 491524

commit v4 on v3

--- a/solution.py
+++ b/solution.py
@@ -217,6 +217,7 @@
 
 MESH = pl.DeviceIdType.MESH
 VMEM_LIMIT = 40000 * 1024
+GROUP = 1
 
 
 def split(value):
@@ -333,32 +334,32 @@
     ends = cuts_of(slots_k)
     chunks = list(zip([0] + ends[:-1], ends))
 
+    sources = (
+        occ_res_hbm, species_hbm, corner_hbm, xf_hbm,
+        occ_hbm, dens_hbm, yt_hbm, zf_hbm, zb_hbm, xb_hbm,
+    )
+    targets = (
+        occ_res_ref, species_ref, corner_ref, xf_ref,
+        occ_ref, dens, yt_ref, zf_ref, zb_ref, xb_ref,
+    )
+    loads = [
+        pltpu.make_async_copy(a, b, table_sem.at[at])
+        for at, (a, b) in enumerate(zip(sources, targets))
+    ]
+
+    def res_load(z):
+        return pltpu.make_async_copy(res_hbm.at[:, z], res.at[:, z], res_sem.at[z])
+
+    res_loads = [res_load(z) for z in range(z_local)]
+    for copy in res_loads[:-1] + loads[:3] + res_loads[-1:] + loads[3:4]:
+        copy.start()
+
     partners = []
     for step in range(1, devices):
         across = pencil + step % pencils
         row = lax.rem(slab + step // pencils + lax.div(across, pencils), slabs)
         column = lax.rem(across, pencils)
         partners.append(((row, column), row * pencils + column))
-
-    sources = (
-        occ_res_hbm, species_hbm, corner_hbm, xf_hbm,
-        occ_hbm, dens_hbm, yt_hbm, zf_hbm, zb_hbm, xb_hbm,
-    )
-    targets = (
-        occ_res_ref, species_ref, corner_ref, xf_ref,
-        occ_ref, dens, yt_ref, zf_ref, zb_ref, xb_ref,
-    )
-    loads = [
-        pltpu.make_async_copy(a, b, table_sem.at[at])
-        for at, (a, b) in enumerate(zip(sources, targets))
-    ]
-
-    def res_load(z):
-        return pltpu.make_async_copy(res_hbm.at[:, z], res.at[:, z], res_sem.at[z])
-
-    res_loads = [res_load(z) for z in range(z_local)]
-    for copy in loads[1:3] + res_loads[:-1] + loads[:1] + res_loads[-1:] + loads[3:4]:
-        copy.start()
 
     barrier = pltpu.get_barrier_semaphore()
 
@@ -631,14 +632,22 @@
 
 
 def finish_kernel(last, dens_ref, occ_ref, xb_ref, out_hbm, occ_hbm, out_ref, sem):
-    tiles = last.shape[0]
-    table = (xb_ref[0], xb_ref[1])
+    tiles, depth, _ = last.shape
     copies = [pltpu.make_async_copy(occ_ref, occ_hbm, sem.at[tiles])]
     copies[0].start()
-    for t in range(tiles):
-        rows = slice(t * 128, (t + 1) * 128)
-        out_ref[rows, :] = dens_ref[rows, :] + three(split(last[t]), table, ((0,), (0,)))
-        copies.append(pltpu.make_async_copy(out_ref.at[rows], out_hbm.at[rows], sem.at[t]))
+    dot = functools.partial(
+        lax.dot_general,
+        dimension_numbers=(((0,), (0,)), ((), ())),
+        preferred_element_type=jnp.float32,
+    )
+    for first in range(0, tiles, GROUP):
+        end = min(first + GROUP, tiles)
+        high, low = split(jnp.concatenate([last[t] for t in range(first, end)], axis=1))
+        both = jnp.concatenate((high, low), axis=0)
+        turned = dot(both, xb_ref[:2 * depth]) + dot(high, xb_ref[2 * depth:])
+        rows = slice(first * 128, end * 128)
+        out_ref[rows, :] = dens_ref[rows, :] + turned
+        copies.append(pltpu.make_async_copy(out_ref.at[rows], out_hbm.at[rows], sem.at[first]))
         copies[-1].start()
     for copy in copies:
         copy.wait()
@@ -713,7 +722,7 @@
         out_specs=(hbm, hbm),
         scratch_shapes=[pltpu.VMEM(flat.shape, flat.dtype), sems((tiles + 1,))],
         compiler_params=pltpu.CompilerParams(vmem_limit_bytes=8 * 1024 * 1024),
-    )(last, mixed, mixed_blocks, jnp.asarray(x_back[:, late:]))
+    )(last, mixed, mixed_blocks, jnp.asarray(np.concatenate((x_back[0, late:], *x_back[:, late:]))))
     return new_density.reshape(z_local, y_local, x_length), new_blocks
 
 

time: 49.6 us -> 49.5 us (level)
  no operation moved by 1% of the time
where the time goes in v4:
time: 49.5 us; the launch traced here: 49.3 us
  Pallas kernels  48 us (97%)
  between operations  1.3 us (3%)
    pallas_call x1, Pallas kernels, fused_body(): pl.pallas_call(functools.partial(mix_kernel, slabs, pencils, z_length * y...  46.8 us
    pallas_call x1, Pallas kernels, fused_body(): pl.pallas_call(finish_kernel, out_shape=(flat, blocks), in_specs=[vmem] *...  1.26 us

profile of v4, /device:TPU:25, one launch (start us, length us, event | category | flops | bytes accessed | tf_op | source)
XLA Modules:
  0.0 49.3 jit_solution(17049098182531743528)
XLA Ops:
  1.3 0.0 copy-start
  1.3 46.8 %shard_map.140 = (f32[640,320]{1,0:T(8,128)S(1)}, f32[24,324]{1,0:T(8,128)S(1)}, f32[5,128,128]{2,1,0:T(8,128)S(1)}) custom-call(s32[1]{0:T(128)S(6)} %copy.15.live_ref, f32[7,8,80,320]{3,2,1,0:T(8,128)} %res_hbm.1, f32[7,8,80,320]{3,2,1,0:T(8,128)} %dens_hbm.1, f32[7,24,324]{2,1,0:T(8,128)} %occ_hbm.1, f32[7,24,324]{2,1,0:T(8,128)} %occ_res_hbm.1, ...), custom_call_target="tpu_custom_call" | custom-call | tf_op jit(solution)/shard_map/pallas_call | solution.py:683
  48.1 0.0 copy-done
  48.1 1.3 %shard_map.141 = (f32[640,320]{1,0:T(8,128)}, f32[24,324]{1,0:T(8,128)}) custom-call(f32[5,128,128]{2,1,0:T(8,128)S(1)} %get-tuple-element.7.last, f32[640,320]{1,0:T(8,128)S(1)} %get-tuple-element.8.dens_ref, f32[24,324]{1,0:T(8,128)S(1)} %get-tuple-element.9.occ_ref, bf16[384,320]{1,0:T(8,128)(2,1)S(1)} %copy-done), custom_call_target="tpu_custom_call" | custom-call | tf_op jit(solution)/shard_map/pallas_call | solution.py:718
Async XLA Ops:
  1.3 46.8 %copy-start = (bf16[384,320]{1,0:T(8,128)(2,1)S(1)}, bf16[384,320]{1,0:T(8,128)(2,1)}, u32[]{:S(2)}) copy-start(bf16[384,320]{1,0:T(8,128)(2,1)} %constant.20.clone.xb_ref) | copy-start | bytes 737284

commit v5 on v4

--- a/solution.py
+++ b/solution.py
@@ -347,11 +347,24 @@
         for at, (a, b) in enumerate(zip(sources, targets))
     ]
 
-    def res_load(z):
-        return pltpu.make_async_copy(res_hbm.at[:, z], res.at[:, z], res_sem.at[z])
-
-    res_loads = [res_load(z) for z in range(z_local)]
-    for copy in res_loads[:-1] + loads[:3] + res_loads[-1:] + loads[3:4]:
+    half = y_local // 16 * 8
+    end_plane = z_local - 1
+
+    def res_load(z, first, size, at):
+        rows = pl.ds(first, size)
+        return pltpu.make_async_copy(
+            res_hbm.at[:, z, rows], res.at[:, z, rows], res_sem.at[at]
+        )
+
+    open_loads = [
+        res_load(0, 0, half, 0), res_load(0, half, y_local - half, z_local)
+    ]
+    res_loads = [res_load(z, 0, y_local, z) for z in range(1, end_plane)]
+    end_loads = [
+        res_load(end_plane, 0, half, end_plane),
+        res_load(end_plane, half, y_local - half, z_local + 1),
+    ]
+    for copy in open_loads + res_loads + loads[:3] + end_loads + loads[3:4]:
         copy.start()
 
     partners = []
@@ -375,18 +388,25 @@
     def lanes_of(length):
         return [(at, min(at + 128, length)) for at in range(0, length, 128)]
 
-    def plane(z, acc):
+    def add_rows(z, first, end, acc):
         acc = list(acc)
-        res_load(z).wait()
-        for row in range(0, y_local, 8):
+        for row in range(first, end, 8):
             for start, stop in lanes_of(x_length):
                 part = [wide(res[i, z, row:row + 8, start:stop]) for i in range(count)]
                 for at, (i, j) in enumerate(pairs):
                     acc[at] = acc[at] + part[i] * part[j]
         return tuple(acc)
 
+    def plane(z, acc):
+        res_load(z, 0, y_local, z).wait()
+        return add_rows(z, 0, y_local, acc)
+
     nothing = tuple(jnp.zeros((8, 128), jnp.float32) for _ in pairs)
-    acc = lax.fori_loop(0, z_local - 1, plane, nothing)
+    open_loads[0].wait()
+    acc = add_rows(0, 0, half, nothing)
+    open_loads[1].wait()
+    acc = add_rows(0, half, y_local, acc)
+    acc = lax.fori_loop(1, end_plane, plane, acc)
     for copy in loads[:3]:
         copy.wait()
     slot_count, entries = occ_ref.shape[1:]
@@ -413,7 +433,10 @@
             for at, (i, j) in enumerate(pairs):
                 blocks_acc[at] = blocks_acc[at] + part[i] * part[j]
     acc = [value + blocks * ratio for value, blocks in zip(acc, blocks_acc)]
-    acc = plane(z_local - 1, acc)
+    end_loads[0].wait()
+    acc = add_rows(end_plane, 0, half, acc)
+    end_loads[1].wait()
+    acc = add_rows(end_plane, half, y_local, acc)
 
     for copy in loads[4:]:
         copy.start()
@@ -701,7 +724,7 @@
             pltpu.VMEM(box, jnp.float32),
             pltpu.VMEM((box[0], late or 16, 128), jnp.float32),
             *[pltpu.VMEM(t.shape, t.dtype) for t in constants],
-            sems((z_local,)),
+            sems((z_local + 2,)),
             sems((5 + len(constants),)),
             sems((2,)),
             sems((1,)), sems((chunks,)),
@@ -745,6 +768,7 @@
             and mesh.shape["slab"] % 8 == 0
             and y_local % 16 == 0
             and z_local * y_local % 128 == 0
+            and z_local > 1
         )
         return (fused_body if fits else body)(*arrays)
 

time: 49.5 us -> 49.5 us (level)
  no operation moved by 1% of the time
where the time goes in v5:
time: 49.5 us; the launch traced here: 49.4 us
  Pallas kernels  48.1 us (97%)
  between operations  1.3 us (3%)
    pallas_call x1, Pallas kernels, fused_body(): pl.pallas_call(functools.partial(mix_kernel, slabs, pencils, z_length * y...  46.8 us
    pallas_call x1, Pallas kernels, fused_body(): pl.pallas_call(finish_kernel, out_shape=(flat, blocks), in_specs=[vmem] *...  1.27 us

profile of v5, /device:TPU:25, one launch (start us, length us, event | category | flops | bytes accessed | tf_op | source)
XLA Modules:
  0.0 49.4 jit_solution(11743369567665852249)
XLA Ops:
  1.3 0.0 copy-start
  1.3 46.8 %shard_map.140 = (f32[640,320]{1,0:T(8,128)S(1)}, f32[24,324]{1,0:T(8,128)S(1)}, f32[5,128,128]{2,1,0:T(8,128)S(1)}) custom-call(s32[1]{0:T(128)S(6)} %copy.15.live_ref, f32[7,8,80,320]{3,2,1,0:T(8,128)} %res_hbm.1, f32[7,8,80,320]{3,2,1,0:T(8,128)} %dens_hbm.1, f32[7,24,324]{2,1,0:T(8,128)} %occ_hbm.1, f32[7,24,324]{2,1,0:T(8,128)} %occ_res_hbm.1, ...), custom_call_target="tpu_custom_call" | custom-call | tf_op jit(solution)/shard_map/pallas_call | solution.py:706
  48.1 0.0 copy-done
  48.1 1.3 %shard_map.141 = (f32[640,320]{1,0:T(8,128)}, f32[24,324]{1,0:T(8,128)}) custom-call(f32[5,128,128]{2,1,0:T(8,128)S(1)} %get-tuple-element.7.last, f32[640,320]{1,0:T(8,128)S(1)} %get-tuple-element.8.dens_ref, f32[24,324]{1,0:T(8,128)S(1)} %get-tuple-element.9.occ_ref, bf16[384,320]{1,0:T(8,128)(2,1)S(1)} %copy-done), custom_call_target="tpu_custom_call" | custom-call | tf_op jit(solution)/shard_map/pallas_call | solution.py:741
Async XLA Ops:
  1.3 46.8 %copy-start = (bf16[384,320]{1,0:T(8,128)(2,1)S(1)}, bf16[384,320]{1,0:T(8,128)(2,1)}, u32[]{:S(2)}) copy-start(bf16[384,320]{1,0:T(8,128)(2,1)} %constant.20.clone.xb_ref) | copy-start | bytes 737284
